TPU v7x, 32 devices: a whole 2x2x4 slice. The times are simulated.
32 devices in a mesh: dp: 4 (over z), expert: 8 (over y, x, core).
Axes of the slice: x: 2, y: 2, z: 4, core: 2. Of those that a mesh axis runs over, the one named last changes fastest.
Arguments:
- tokens: bfloat16 [512, 7168], P('expert'), may hold values from -6 to 6
- routes: int32 [512, 8], P('expert'), may hold values from 0 to 7, all different within a row; in each aligned block of 64 rows (0 to 63, 64 to 127, ...) at most 64 rows name the same one
- route_weight: int32 [512, 8], P('expert'), may hold values from 1 to 4096
- w_gate: bfloat16 [8, 7168, 2048], P('expert', None, 'dp'), may hold values from -0.0625 to 0.0625
- w_up: bfloat16 [8, 7168, 2048], P('expert', None, 'dp'), may hold values from -0.0625 to 0.0625
- w_down: bfloat16 [8, 2048, 7168], P('expert', 'dp'), may hold values from -0.125 to 0.125
- prev_inputs: bfloat16 [4, 8, 64, 7168], P('dp', 'expert'), may hold values from -6 to 6
Outputs:
- mixed: bfloat16 [512, 7168], P('expert', 'dp')
- hessian: float32 [7168, 8, 128], P('dp', 'expert')
Inputs may be any that keep to these rules, and one draw needn't show every extreme that they name: `routes`: in each aligned block of 64 rows (the rows of one index of expert) no expert is named more than 64 times, a bound that some block reaches; the 8 experts of a token differ.
All inputs are finite; a program needn't handle non-finite values.
Results may differ from a plain program's by a relative error of at most 0.014.
Values may be sent and summed in bfloat16 or wider, within the bound.
A program may use at most 128 MiB of HBM per device.

v0:
```python
import functools

import jax
import jax.numpy as jnp
from jax import lax
from jax.experimental import pallas as pl
from jax.experimental.pallas import tpu as pltpu
from jax.sharding import PartitionSpec as P

HESS_COLS = 128


def route_slots(flat_ids, experts_all):
    onehot = (flat_ids[:, None] == jnp.arange(experts_all, dtype=jnp.int32)[None, :]).astype(
        jnp.int32
    )
    earlier = jnp.cumsum(onehot, axis=0) - onehot
    return jnp.sum(earlier * onehot, axis=1)


def combine_rows(back, places, shares, tok_dev, top):
    columns = back.shape[-1]
    rows = back.reshape(-1, columns)[places]
    weighted = rows.astype(jnp.float32) * shares.reshape(-1, 1)
    return jnp.sum(weighted.reshape(tok_dev, top, columns), axis=1)


def route_shares(route_weight):
    weight_counts = route_weight.astype(jnp.float32)
    return 2.5 * weight_counts / jnp.sum(weight_counts, axis=1, keepdims=True)


def gram_window(prev_inputs, n_dp, width):
    history = prev_inputs.reshape(prev_inputs.shape[1], prev_inputs.shape[2], width)
    head_cols = history[:, :, :HESS_COLS]
    gram_scale = 2.0 / (n_dp * history.shape[1])
    return lax.psum_scatter(
        (
            jnp.einsum("jrd,jrh->djh", history, head_cols, preferred_element_type=jnp.float32)
            * gram_scale
        ).astype(jnp.bfloat16),
        "dp",
        scatter_dimension=0,
        tiled=True,
    ).astype(jnp.float32)


def slotted(tokens, routes, route_weight, w_gate, w_up, w_down):
    tok_dev, top = routes.shape
    exp_dev = w_gate.shape[0]
    width = tokens.shape[1]
    n_expert = lax.axis_size("expert")
    experts_all = exp_dev * n_expert
    capacity = min(tok_dev, tok_dev * top * 5 // (4 * experts_all))
    flat_ids = routes.reshape(-1)
    slots = route_slots(flat_ids, experts_all)
    places = flat_ids * capacity + slots
    shares = route_shares(route_weight)
    picks = jnp.arange(experts_all * capacity, dtype=jnp.int32)[:, None] == places[None, :]
    placing = jnp.any(picks.reshape(experts_all * capacity, tok_dev, top), axis=2).astype(
        jnp.bfloat16
    )
    outgoing = jnp.dot(placing, tokens, preferred_element_type=jnp.float32).astype(jnp.bfloat16)
    outgoing = outgoing.reshape(experts_all, capacity, width)
    arrived = lax.all_to_all(outgoing, "expert", split_axis=0, concat_axis=0, tiled=True)
    arrived = arrived.reshape(n_expert, exp_dev, capacity, width)
    gate = jnp.einsum("sjcd,jdf->sjcf", arrived, w_gate, preferred_element_type=jnp.float32)
    up = jnp.einsum("sjcd,jdf->sjcf", arrived, w_up, preferred_element_type=jnp.float32)
    hidden = (jax.nn.silu(gate) * up).astype(jnp.bfloat16)
    partial_out = jnp.einsum("sjcf,jfd->sjcd", hidden, w_down, preferred_element_type=jnp.float32)
    partial_out = partial_out.astype(jnp.bfloat16)
    back = lax.all_to_all(
        partial_out.reshape(experts_all, capacity, width),
        "expert",
        split_axis=0,
        concat_axis=0,
        tiled=True,
    )
    own_sum = combine_rows(back, places, shares, tok_dev, top)
    return lax.psum_scatter(own_sum.astype(jnp.bfloat16), "dp", scatter_dimension=1, tiled=True)

LANES = 128
MESH = pl.DeviceIdType.MESH


def flip(index, bit):
    return index + bit - 2 * bit * ((index // bit) % 2)


def dense_kernel(
    n_dp,
    n_expert,
    tokens,
    share_in,
    w_gate,
    w_up,
    w_down,
    prev,
    mixed_ref,
    hess_ref,
    xall,
    share_all,
    wg,
    wu,
    wd,
    g_acc,
    u_acc,
    hid,
    mine,
    sb0,
    rb0,
    sb1,
    rb1,
    sb2,
    rb2,
    sb3,
    rb3,
    hx,
    hh,
    lsem,
    send_sem,
    recv_sem,
):
    me = lax.axis_index("expert")
    my_dp = lax.axis_index("dp")
    core, xx, yy = me % 2, (me // 2) % 2, (me // 4) % 2
    peer, ex, ey = flip(me, 1), flip(me, 2), flip(me, 4)
    ed = flip(ex, 4)
    chunks, depth = xall.shape[0], xall.shape[-1]
    rows = xall.shape[3]
    half = rows // 2
    cols = rb3.shape[-1]
    hidden_w = wg.shape[-1]
    counter = [0]
    local_counter = [0]

    def local(src, dst):
        copy = pltpu.make_async_copy(src, dst, lsem.at[local_counter[0]])
        local_counter[0] += 1
        copy.start()
        return copy

    def remote(src, dst, where):
        copy = pltpu.make_async_remote_copy(
            src_ref=src,
            dst_ref=dst,
            send_sem=send_sem.at[counter[0]],
            recv_sem=recv_sem.at[counter[0]],
            device_id=where,
            device_id_type=MESH,
        )
        counter[0] += 1
        copy.start()
        sent.append(copy)
        return copy

    sent = []
    side = my_dp % 2
    last = chunks - 1

    def piece(c):
        return pl.ds(pl.multiple_of((side * last + c * (1 - 2 * side)) * depth, LANES), depth)

    token_loads = [
        local(tokens.at[:, piece(c)], xall.at[c, core, me // 2]) for c in range(chunks)
    ]
    hist_own = local(prev.at[:, pl.ds(pl.multiple_of(my_dp * cols, LANES), cols)], hx.at[0])
    head_own = local(prev.at[:, 0:HESS_COLS], hh.at[0])
    share_own = local(share_in, share_all.at[core, me // 2])
    gate_loads, up_loads = [], []
    for c in range(chunks):
        gate_loads.append(local(w_gate.at[piece(c), :], wg.at[c]))
        up_loads.append(local(w_up.at[piece(c), :], wu.at[c]))
    turns = [n_dp // 2] + [d for d in range(1, n_dp) if d != n_dp // 2] + [0]
    down_loads = []
    for i, d in enumerate(turns):
        start = pl.multiple_of(((my_dp + d) % n_dp) * cols, LANES)
        down_loads.append(local(w_down.at[:, pl.ds(start, cols)], wd.at[i]))

    barrier = pltpu.get_barrier_semaphore()
    for d in range(1, n_expert):
        pl.semaphore_signal(
            barrier, inc=1, device_id={"expert": (me + d) % n_expert}, device_id_type=MESH
        )
    for d in range(1, n_dp):
        pl.semaphore_signal(
            barrier, inc=1, device_id={"dp": (my_dp + d) % n_dp}, device_id_type=MESH
        )
    pl.semaphore_wait(barrier, n_expert + n_dp - 2)

    to_z = {"dp": flip(my_dp, 1)}
    to_peer, to_x, to_y = {"expert": peer}, {"expert": ex}, {"expert": ey}
    flow = {}

    def block(c, who):
        return xall.at[c, who % 2, who // 2]

    def own(c):
        token_loads[c].wait()
        ways = (("x", to_x), ("y", to_y), ("p", to_peer))
        for name, where in ways if c < last else ways[2:]:
            flow[c, name] = remote(block(c, me), block(c, me), where)

    def across(who):
        return remote(block(0, who), block(last, who), to_z)

    def relay(c):
        if c == last:
            for name, who in (("x", ex), ("y", ey), ("d", ed)):
                flow["z" + name].wait_recv()
                flow[c, "p" + name] = remote(block(c, who), block(c, who), to_peer)
            return
        flow[c, "x"].wait_recv()
        flow[c, "d0"] = remote(block(c, ex).at[0:half], block(c, ex).at[0:half], to_y)
        if c == 0:
            flow["zx"] = across(ex)
        flow[c, "px"] = remote(block(c, ex), block(c, ex), to_peer)
        flow[c, "y"].wait_recv()
        flow[c, "d1"] = remote(block(c, ey).at[half:rows], block(c, ey).at[half:rows], to_x)
        if c == 0:
            flow["zy"] = across(ey)
        flow[c, "py"] = remote(block(c, ey), block(c, ey), to_peer)

    def corner(c):
        if c == last:
            return
        flow[c, "d0"].wait_recv()
        flow[c, "p0"] = remote(block(c, ed).at[0:half], block(c, ed).at[0:half], to_peer)
        flow[c, "d1"].wait_recv()
        flow[c, "p1"] = remote(block(c, ed).at[half:rows], block(c, ed).at[half:rows], to_peer)
        if c == 0:
            flow["zd"] = across(ed)

    tile = 2 * LANES

    def widen(c):
        for name in ("p", "px", "py", "p0", "p1") if c < last else ("p", "px", "py", "pd"):
            flow[c, name].wait_recv()
        gate_loads[c].wait()
        up_loads[c].wait()

        @pl.loop(0, hidden_w // tile)
        def _(n):
            at = pl.ds(pl.multiple_of(n * tile, tile), tile)
            x = xall[c].reshape(n_expert * rows, depth)
            g = jnp.dot(x, wg[c, :, at], preferred_element_type=jnp.float32)
            u = jnp.dot(x, wu[c, :, at], preferred_element_type=jnp.float32)
            if c == 0:
                g_acc[:, at] = g
                u_acc[:, at] = u
            else:
                g_acc[:, at] += g
                u_acc[:, at] += u

    own(0)
    share_own.wait()
    share_flows = [
        remote(
            share_all.at[core, me // 2],
            share_all.at[core, me // 2],
            {"expert": (me + d) % n_expert},
        )
        for d in range(1, n_expert)
    ]
    hist_flows = []

    def send_history():
        for d in range(1, n_dp):
            start = pl.multiple_of(((my_dp + d) % n_dp) * cols, LANES)
            where = {"dp": (my_dp + d) % n_dp}
            hist_flows.append(remote(prev.at[:, pl.ds(start, cols)], hx.at[d], where))
            hist_flows.append(remote(prev.at[:, 0:HESS_COLS], hh.at[d], where))

    for c in range(chunks + 2):
        if 1 <= c < chunks:
            own(c)
        if 1 <= c <= chunks:
            relay(c - 1)
        if 2 <= c:
            corner(c - 2)
            if c == 2:
                send_history()
            widen(c - 2)

    for copy in share_flows:
        copy.wait_recv()
    for kind in range(2):
        span = slice(kind * n_expert // 2 * rows, (kind + 1) * n_expert // 2 * rows)
        sh = share_all[kind].reshape(n_expert // 2 * rows, LANES)
        lane = lax.broadcasted_iota(jnp.int32, sh.shape, 1)
        own_share = jnp.sum(jnp.where(lane == me, sh, 0.0), axis=1, keepdims=True)
        g = g_acc[span, :]
        hid[kind] = (g / (1.0 + jnp.exp(-g)) * u_acc[span, :] * own_share).astype(jnp.bfloat16)

    stage = {}
    chips = n_expert // 2

    def down(i):
        down_loads[i].wait()

        @pl.loop(0, cols // tile)
        def _(n):
            at = pl.ds(pl.multiple_of(n * tile, tile), tile)
            out = jnp.dot(hid[1 - core], wd[i, :, at], preferred_element_type=jnp.float32)
            sb0[i, :, :, at] = out.astype(jnp.bfloat16).reshape(chips, rows, tile)

        stage[i, 0] = remote(sb0.at[i], rb0.at[i], to_peer)

    def keep(i):
        @pl.loop(0, cols // tile)
        def _(n):
            at = pl.ds(pl.multiple_of(n * tile, tile), tile)
            out = jnp.dot(hid[core], wd[i, :, at], preferred_element_type=jnp.float32)
            mine[i, :, :, at] = out.reshape(chips, rows, tile)

    low, high = slice(0, half), slice(half, rows)

    def both(i, chip, part):
        return mine[i, chip, part, :] + rb0[i, chip, part, :].astype(jnp.float32)

    def first(i):
        stage[i, 0].wait_recv()
        for k in range(2):
            sb1[i, 0, k] = both(i, k * 2 + 1 - xx, low).astype(jnp.bfloat16)
        stage[i, 1] = remote(sb1.at[i, 0], rb1.at[i, 0], to_x)
        for k in range(2):
            sb1[i, 1, k] = both(i, (1 - yy) * 2 + k, high).astype(jnp.bfloat16)
        stage[i, 2] = remote(sb1.at[i, 1], rb1.at[i, 1], to_y)

    def second(i):
        stage[i, 1].wait_recv()
        out = both(i, (1 - yy) * 2 + xx, low) + rb1[i, 0, 1 - yy].astype(jnp.float32)
        sb2[i, 0] = out.astype(jnp.bfloat16)
        stage[i, 3] = remote(sb2.at[i, 0], rb2.at[i, 0], to_y)
        stage[i, 2].wait_recv()
        out = both(i, yy * 2 + 1 - xx, high) + rb1[i, 1, 1 - xx].astype(jnp.float32)
        sb2[i, 1] = out.astype(jnp.bfloat16)
        stage[i, 4] = remote(sb2.at[i, 1], rb2.at[i, 1], to_x)

    def third(i):
        d = turns[i]
        chip = me // 2
        stage[i, 3].wait_recv()
        stage[i, 4].wait_recv()
        top = both(i, chip, low) + rb1[i, 0, yy].astype(jnp.float32)
        top = top + rb2[i, 0].astype(jnp.float32)
        end = both(i, chip, high) + rb1[i, 1, xx].astype(jnp.float32)
        end = end + rb2[i, 1].astype(jnp.float32)
        if d:
            sb3[d - 1, low, :] = top.astype(jnp.bfloat16)
            sb3[d - 1, high, :] = end.astype(jnp.bfloat16)
            stage[i, 5] = remote(
                sb3.at[d - 1], rb3.at[d - 1], {"dp": (my_dp + d) % n_dp}
            )
        else:
            for j, other in enumerate(turns):
                if other:
                    stage[j, 5].wait_recv()
                    top = top + rb3[other - 1, low, :].astype(jnp.float32)
                    end = end + rb3[other - 1, high, :].astype(jnp.float32)
            mixed_ref[low, :] = top.astype(jnp.bfloat16)
            mixed_ref[high, :] = end.astype(jnp.bfloat16)

    def gram():
        hist_own.wait()
        head_own.wait()
        for copy in hist_flows:
            copy.wait_recv()
        scale = 2.0 / (n_dp * hx.shape[1])

        @pl.loop(0, cols // tile)
        def _(n):
            at = pl.multiple_of(n * tile, tile)
            left = hx[:, :, pl.ds(at, tile)].reshape(n_dp * hx.shape[1], tile)
            right = hh[...].reshape(n_dp * hx.shape[1], HESS_COLS)
            product = lax.dot_general(
                left, right, (((0,), (0,)), ((), ())), preferred_element_type=jnp.float32
            )
            hess_ref[pl.ds(at, tile), :] = product * scale

    for step in range(n_dp + 4):
        if step < n_dp:
            down(step)
        if 1 <= step <= n_dp:
            keep(step - 1)
            first(step - 1)
        if step == n_dp + 1:
            gram()
        if 3 <= step < n_dp + 3:
            second(step - 3)
        if 4 <= step:
            third(step - 4)
    for copy in sent:
        copy.wait_send()


def everyone(tokens, routes, route_weight, w_gate, w_up, w_down, prev_inputs):
    rows, width = tokens.shape
    n_expert = lax.axis_size("expert")
    n_dp = lax.axis_size("dp")
    hidden_w = w_gate.shape[2]
    shares = route_shares(route_weight)
    named = routes[:, :, None] == jnp.arange(LANES, dtype=jnp.int32)[None, None, :]
    by_expert = jnp.sum(jnp.where(named, shares[:, :, None], 0.0), axis=1)
    prev = prev_inputs.reshape(prev_inputs.shape[2], width)
    cols = width // n_dp
    chunks = 4
    depth = width // chunks
    chips = n_expert // 2
    total = n_expert * rows
    bf16, f32 = jnp.bfloat16, jnp.float32
    copies = 9 * chunks + (n_expert - 1) + 2 * (n_dp - 1) + 5 * n_dp + n_dp - 1
    vmem = pl.BlockSpec(memory_space=pltpu.VMEM)
    hbm = pl.BlockSpec(memory_space=pl.ANY)
    mixed, hess = pl.pallas_call(
        functools.partial(dense_kernel, n_dp, n_expert),
        out_shape=(
            jax.ShapeDtypeStruct((rows, cols), bf16),
            jax.ShapeDtypeStruct((cols, HESS_COLS), f32),
        ),
        in_specs=[hbm] * 6,
        out_specs=(vmem, vmem),
        scratch_shapes=[
            pltpu.VMEM((chunks, 2, chips, rows, depth), bf16),
            pltpu.VMEM((2, chips, rows, LANES), f32),
            pltpu.VMEM((chunks, depth, hidden_w), bf16),
            pltpu.VMEM((chunks, depth, hidden_w), bf16),
            pltpu.VMEM((n_dp, hidden_w, cols), bf16),
            pltpu.VMEM((total, hidden_w), f32),
            pltpu.VMEM((total, hidden_w), f32),
            pltpu.VMEM((2, total // 2, hidden_w), bf16),
            pltpu.VMEM((n_dp, chips, rows, cols), f32),
            pltpu.VMEM((n_dp, chips, rows, cols), bf16),
            pltpu.VMEM((n_dp, chips, rows, cols), bf16),
            pltpu.VMEM((n_dp, 2, 2, rows // 2, cols), bf16),
            pltpu.VMEM((n_dp, 2, 2, rows // 2, cols), bf16),
            pltpu.VMEM((n_dp, 2, rows // 2, cols), bf16),
            pltpu.VMEM((n_dp, 2, rows // 2, cols), bf16),
            pltpu.VMEM((n_dp - 1, rows, cols), bf16),
            pltpu.VMEM((n_dp - 1, rows, cols), bf16),
            pltpu.VMEM((n_dp, prev.shape[0], cols), bf16),
            pltpu.VMEM((n_dp, prev.shape[0], HESS_COLS), bf16),
            pltpu.SemaphoreType.DMA((3 * chunks + n_dp + 3,)),
            pltpu.SemaphoreType.DMA((copies,)),
            pltpu.SemaphoreType.DMA((copies,)),
        ],
        compiler_params=pltpu.CompilerParams(
            collective_id=0, has_side_effects=True, vmem_limit_bytes=67043328
        ),
        name="dense_layer",
    )(tokens, by_expert, w_gate[0], w_up[0], w_down[0], prev)
    return mixed, hess.reshape(cols, 1, HESS_COLS)


def shards(tokens, routes, route_weight, w_gate, w_up, w_down, prev_inputs):
    n_expert = lax.axis_size("expert")
    if w_gate.shape[0] == 1 and routes.shape[1] == n_expert == 2 * 2 * 2:
        return everyone(tokens, routes, route_weight, w_gate, w_up, w_down, prev_inputs)
    hessian = gram_window(prev_inputs, lax.axis_size("dp"), tokens.shape[1])
    return slotted(tokens, routes, route_weight, w_gate, w_up, w_down), hessian


def solution(mesh):
    placed = (
        P("expert", None),
        P("expert", None),
        P("expert", None),
        P("expert", None, "dp"),
        P("expert", None, "dp"),
        P("expert", "dp", None),
        P("dp", "expert", None, None),
    )
    return jax.shard_map(
        shards,
        mesh=mesh,
        in_specs=placed,
        out_specs=(P("expert", "dp"), P("dp", "expert", None)),
        check_vma=False,
    )
```

profile of v0, /device:TPU:0, one launch (start us, length us, event | category | flops | bytes accessed | tf_op | source)
XLA Modules:
  0.0 96.3 jit_solution(10830275046982386166)
XLA Ops:
  0.6 0.7 convert_reduce_fusion
  1.3 0.7 multiply_divide_fusion
  2.0 0.1 copy.13
  2.1 0.8 copy.12
  2.9 0.8 select_reduce_fusion.share_in
  3.7 89.0 %dense_layer.1 = (bf16[64,1792]{1,0:T(8,128)(2,1)}, f32[1792,128]{1,0:T(8,128)}) custom-call(bf16[64,7168]{1,0:T(8,128)(2,1)} %tokens.1, f32[64,128]{1,0:T(8,128)} %select_reduce_fusion.share_in, bf16[7168,512]{1,0:T(8,128)(2,1)} %bitcast.7, bf16[7168,512]{1,0:T(8,128)(2,1)} %bitcast.8, bf16[512,7168]{1,0:T(8,128)(2,1)} %bitcast.9, bf16[64,7168]{1,0:T(8,128)(2,1)} %bitcast.11), custom_call_target="tpu_custom_call" | custom-call | tf_op jit(solution)/shard_map/dense_layer/pallas_call | solution.py:415
  92.7 1.6 %copy.17 = bf16[64,1792]{1,0:T(8,128)(2,1)} copy(bf16[64,1792]{1,0:T(8,128)(2,1)} %get-tuple-element.12) | data formatting | bytes 458752
  94.4 2.0 %copy.18 = f32[1792,1,128]{2,1,0:T(1,128)} copy(f32[1792,1,128]{2,1,0:T(1,128)} %bitcast.10) | data formatting | bytes 1835008
where the time goes:
time: 96.8 us; the launch traced here: 96.3 us
  Pallas kernels  89 us (92%)
  local copies, waits for them, and re-layouts  4.47 us (5%)
  other arithmetic  2.22 us (2%)
    pallas_call x1, Pallas kernels, everyone(): pl.pallas_call(functools.partial(dense_kernel, n_dp, n_expert), out_shape...  89 us
    unnamed x3, local copies, waits for them, and re-layouts  4.38 us

commit v1 on v0

v1 whole, which is shorter than its diff:
```python
import functools

import jax
import jax.numpy as jnp
from jax import lax
from jax.experimental import pallas as pl
from jax.experimental.pallas import tpu as pltpu
from jax.sharding import PartitionSpec as P

HESS_COLS = 128


def route_slots(flat_ids, experts_all):
    onehot = (flat_ids[:, None] == jnp.arange(experts_all, dtype=jnp.int32)[None, :]).astype(
        jnp.int32
    )
    earlier = jnp.cumsum(onehot, axis=0) - onehot
    return jnp.sum(earlier * onehot, axis=1)


def combine_rows(back, places, shares, tok_dev, top):
    columns = back.shape[-1]
    rows = back.reshape(-1, columns)[places]
    weighted = rows.astype(jnp.float32) * shares.reshape(-1, 1)
    return jnp.sum(weighted.reshape(tok_dev, top, columns), axis=1)


def route_shares(route_weight):
    weight_counts = route_weight.astype(jnp.float32)
    return 2.5 * weight_counts / jnp.sum(weight_counts, axis=1, keepdims=True)


def gram_window(prev_inputs, n_dp, width):
    history = prev_inputs.reshape(prev_inputs.shape[1], prev_inputs.shape[2], width)
    head_cols = history[:, :, :HESS_COLS]
    gram_scale = 2.0 / (n_dp * history.shape[1])
    return lax.psum_scatter(
        (
            jnp.einsum("jrd,jrh->djh", history, head_cols, preferred_element_type=jnp.float32)
            * gram_scale
        ).astype(jnp.bfloat16),
        "dp",
        scatter_dimension=0,
        tiled=True,
    ).astype(jnp.float32)


def slotted(tokens, routes, route_weight, w_gate, w_up, w_down):
    tok_dev, top = routes.shape
    exp_dev = w_gate.shape[0]
    width = tokens.shape[1]
    n_expert = lax.axis_size("expert")
    experts_all = exp_dev * n_expert
    capacity = min(tok_dev, tok_dev * top * 5 // (4 * experts_all))
    flat_ids = routes.reshape(-1)
    slots = route_slots(flat_ids, experts_all)
    places = flat_ids * capacity + slots
    shares = route_shares(route_weight)
    picks = jnp.arange(experts_all * capacity, dtype=jnp.int32)[:, None] == places[None, :]
    placing = jnp.any(picks.reshape(experts_all * capacity, tok_dev, top), axis=2).astype(
        jnp.bfloat16
    )
    outgoing = jnp.dot(placing, tokens, preferred_element_type=jnp.float32).astype(jnp.bfloat16)
    outgoing = outgoing.reshape(experts_all, capacity, width)
    arrived = lax.all_to_all(outgoing, "expert", split_axis=0, concat_axis=0, tiled=True)
    arrived = arrived.reshape(n_expert, exp_dev, capacity, width)
    gate = jnp.einsum("sjcd,jdf->sjcf", arrived, w_gate, preferred_element_type=jnp.float32)
    up = jnp.einsum("sjcd,jdf->sjcf", arrived, w_up, preferred_element_type=jnp.float32)
    hidden = (jax.nn.silu(gate) * up).astype(jnp.bfloat16)
    partial_out = jnp.einsum("sjcf,jfd->sjcd", hidden, w_down, preferred_element_type=jnp.float32)
    partial_out = partial_out.astype(jnp.bfloat16)
    back = lax.all_to_all(
        partial_out.reshape(experts_all, capacity, width),
        "expert",
        split_axis=0,
        concat_axis=0,
        tiled=True,
    )
    own_sum = combine_rows(back, places, shares, tok_dev, top)
    return lax.psum_scatter(own_sum.astype(jnp.bfloat16), "dp", scatter_dimension=1, tiled=True)

LANES = 128
SUBS = 2
MESH = pl.DeviceIdType.MESH


def flip(index, bit):
    return index + bit - 2 * bit * ((index // bit) % 2)


def partner(index, mask):
    bit = 1
    while bit <= mask:
        if mask & bit:
            index = flip(index, bit)
        bit *= 2
    return index


def dense_kernel(
    n_dp,
    n_expert,
    tokens,
    routes,
    route_weight,
    w_gate,
    w_up,
    w_down,
    prev,
    mixed_ref,
    hess_ref,
    xall,
    share_all,
    wg,
    wu,
    wd,
    g_acc,
    u_acc,
    hid,
    mine,
    sb0,
    rb0,
    sb1,
    rb1,
    sb2,
    rb2,
    sb3,
    rb3,
    hx,
    hh,
    ids,
    counts,
    lsem,
    send_sem,
    recv_sem,
):
    me = lax.axis_index("expert")
    my_dp = lax.axis_index("dp")
    core, xx, yy = me % 2, (me // 2) % 2, (me // 4) % 2
    peer, ex, ey = flip(me, 1), flip(me, 2), flip(me, 4)
    ed = flip(ex, 4)
    subs, chunks, depth = xall.shape[0], xall.shape[1], xall.shape[-1]
    rows = xall.shape[4]
    half = rows // 2
    chips = n_expert // 2
    cols = rb3.shape[-1]
    hidden_w = wg.shape[-1]
    tokens_sem, gate_sem, up_sem, down_sem, hist_sem, head_sem, ids_sem, counts_sem = range(8)
    gathers, peers, firsts, seconds, thirds, hists, heads, parts = range(8)
    lanes = {}

    def local(src, dst, sem):
        pltpu.make_async_copy(src, dst, lsem.at[sem]).start()

    def loaded(ref, sem):
        pltpu.make_async_copy(ref, ref, lsem.at[sem]).wait()

    def describe(src, dst, where, group, key):
        return pltpu.make_async_remote_copy(
            src_ref=src,
            dst_ref=dst,
            send_sem=send_sem.at[group],
            recv_sem=recv_sem.at[lanes.setdefault(key, len(lanes))],
            device_id=where,
            device_id_type=MESH,
        )

    def remote(src, dst, where, group, key):
        describe(src, dst, where, group, key).start()

    def arrived(ref, key):
        describe(ref, ref, to_peer, 0, key).wait_recv()

    def departed(ref, group):
        describe(ref, ref, to_peer, group, (0, 0, "x")).wait_send()

    side = my_dp % 2
    last = chunks - 1

    def piece(c):
        return pl.ds(pl.multiple_of((side * last + c * (1 - 2 * side)) * depth, LANES), depth)

    for s in range(subs):
        for c in range(chunks):
            local(
                tokens.at[s * rows : (s + 1) * rows, piece(c)],
                xall.at[s, c, core, me // 2],
                tokens_sem,
            )
    local(routes, ids, ids_sem)
    local(route_weight, counts, counts_sem)
    for c in range(chunks):
        local(w_gate.at[piece(c), :], wg.at[c], gate_sem)
        local(w_up.at[piece(c), :], wu.at[c], up_sem)
    turns = list(range(n_dp - 1, -1, -1))
    for i, d in enumerate(turns):
        start = pl.multiple_of(partner(my_dp, d) * cols, LANES)
        local(w_down.at[:, pl.ds(start, cols)], wd.at[i], down_sem)
    local(prev.at[:, pl.ds(pl.multiple_of(my_dp * cols, LANES), cols)], hx.at[0], hist_sem)
    local(prev.at[:, 0:HESS_COLS], hh.at[0], head_sem)

    barrier = pltpu.get_barrier_semaphore()
    for d in range(1, n_expert):
        pl.semaphore_signal(
            barrier, inc=1, device_id={"expert": (me + d) % n_expert}, device_id_type=MESH
        )
    for d in range(1, n_dp):
        pl.semaphore_signal(
            barrier, inc=1, device_id={"dp": partner(my_dp, d)}, device_id_type=MESH
        )
    pl.semaphore_wait(barrier, n_expert + n_dp - 2)

    to_z = {"dp": flip(my_dp, 1)}
    to_peer, to_x, to_y = {"expert": peer}, {"expert": ex}, {"expert": ey}

    def block(s, c, who):
        return xall.at[s, c, who % 2, who // 2]

    def own(s, c):
        if (s, c) == (0, 0):
            loaded(tokens, tokens_sem)
        here = block(s, c, me)
        if c < last:
            remote(here, here, to_x, gathers, (s, c, "x"))
            remote(here, here, to_y, gathers, (s, c, "y"))
        remote(here, here, to_peer, gathers, (s, c, "p"))

    def share_block(s, c, who):
        remote(block(s, c, who), block(s, c, who), to_peer, gathers, (s, c, "p"))

    def across(s, who):
        remote(block(s, 0, who), block(s, last, who), to_z, gathers, (s, "z"))

    low, high = slice(0, half), slice(half, rows)

    def relay(s, c):
        for name, who, forth, part in (("x", ex, to_y, low), ("y", ey, to_x, high)):
            here = block(s, c, who)
            arrived(here, (s, c, name))
            remote(here.at[part], here.at[part], forth, gathers, (s, c, "d"))
            if c == 0:
                across(s, who)
            share_block(s, c, who)

    def corner(s, c):
        arrived(block(s, c, ed), (s, c, "d"))
        if c == 0:
            across(s, ed)
        share_block(s, c, ed)

    def arrive(s):
        arrived(xall.at[s, last, core, 1:chips], (s, "z"))
        for who in (ex, ey, ed):
            share_block(s, last, who)

    tile = 2 * LANES

    def widen(s, c):
        arrived(xall.at[s, c, 1 - core], (s, c, "p"))
        if (s, c) == (0, 0):
            loaded(wg, gate_sem)
            loaded(wu, up_sem)
        x = xall[s, c].reshape(n_expert * rows, depth)
        for n in range(0, hidden_w, tile):
            at = slice(n, n + tile)
            g = jnp.dot(x, wg[c, :, at], preferred_element_type=jnp.float32)
            u = jnp.dot(x, wu[c, :, at], preferred_element_type=jnp.float32)
            if c == 0:
                g_acc[:, at] = g
                u_acc[:, at] = u
            else:
                g_acc[:, at] += g
                u_acc[:, at] += u

    def send_shares():
        loaded(ids, ids_sem)
        loaded(counts, counts_sem)
        weight = counts[...].astype(jnp.float32)
        part = 2.5 * weight / jnp.sum(weight, axis=0, keepdims=True)
        named = ids[...]
        expert = lax.broadcasted_iota(jnp.int32, (n_expert, named.shape[1]), 0)
        by_expert = jnp.zeros(expert.shape, jnp.float32)
        for k in range(named.shape[0]):
            by_expert += jnp.where(named[k : k + 1, :] == expert, part[k : k + 1, :], 0.0)
        here = share_all.at[core * chips + me // 2]
        here[...] = jnp.zeros((n_expert, LANES), jnp.float32)
        here[:, 0 : named.shape[1]] = by_expert
        for d in range(1, n_expert):
            remote(here, here, {"expert": (me + d) % n_expert}, parts, "shares")

    def history(d):
        start = pl.multiple_of(partner(my_dp, d) * cols, LANES)
        where = {"dp": partner(my_dp, d)}
        remote(prev.at[:, pl.ds(start, cols)], hx.at[d], where, hists, "hist")
        remote(prev.at[:, 0:HESS_COLS], hh.at[d], where, heads, "head")

    def activate(s):
        if s == 0:
            arrived(share_all.at[1:n_expert], "shares")
        table = share_all[...]
        expert = lax.broadcasted_iota(jnp.int32, table.shape, 1)
        table = jnp.sum(jnp.where(expert == me, table, 0.0), axis=1)
        table = jnp.concatenate(
            [table, jnp.zeros((LANES - n_expert, LANES), jnp.float32)], axis=0
        ).T
        for at in range(n_expert):
            kind, chip = at // chips, at % chips
            span = slice(at * rows, (at + 1) * rows)
            own_share = table[s * rows : (s + 1) * rows, at : at + 1]
            g = g_acc[span, :]
            hid[s, (kind + core + 1) % 2, chip * rows : (chip + 1) * rows, :] = (
                g / (1.0 + jnp.exp(-g)) * u_acc[span, :] * own_share
            ).astype(jnp.bfloat16)

    def down(s, i):
        j = s * n_dp + i
        if (s, i) == (0, 0):
            loaded(wd, down_sem)
        h = hid[s].reshape(n_expert * rows, hidden_w)
        for n in range(0, cols, tile):
            at = slice(n, n + tile)
            out = jnp.dot(h, wd[i, :, at], preferred_element_type=jnp.float32)
            out = out.reshape(2, chips, rows, tile)
            sb0[j, :, :, at] = out[0].astype(jnp.bfloat16)
            mine[j, :, :, at] = out[1]
        remote(sb0.at[j], rb0.at[j], to_peer, peers, (s, i, 0))

    def both(j, chip, part):
        return mine[j, chip, part, :] + rb0[j, chip, part, :].astype(jnp.float32)

    def first(s, i):
        j = s * n_dp + i
        arrived(rb0.at[j], (s, i, 0))
        for k in range(2):
            sb1[j, 0, k] = both(j, k * 2 + 1 - xx, low).astype(jnp.bfloat16)
        remote(sb1.at[j, 0], rb1.at[j, 0], to_x, firsts, (s, i, 1))
        for k in range(2):
            sb1[j, 1, k] = both(j, (1 - yy) * 2 + k, high).astype(jnp.bfloat16)
        remote(sb1.at[j, 1], rb1.at[j, 1], to_y, firsts, (s, i, 2))

    def second(s, i):
        j = s * n_dp + i
        arrived(rb1.at[j, 0], (s, i, 1))
        out = both(j, (1 - yy) * 2 + xx, low) + rb1[j, 0, 1 - yy].astype(jnp.float32)
        sb2[j, 0] = out.astype(jnp.bfloat16)
        remote(sb2.at[j, 0], rb2.at[j, 0], to_y, seconds, (s, i, 3))
        arrived(rb1.at[j, 1], (s, i, 2))
        out = both(j, yy * 2 + 1 - xx, high) + rb1[j, 1, 1 - xx].astype(jnp.float32)
        sb2[j, 1] = out.astype(jnp.bfloat16)
        remote(sb2.at[j, 1], rb2.at[j, 1], to_x, seconds, (s, i, 3))

    def third(s, i):
        j = s * n_dp + i
        d = turns[i]
        chip = me // 2
        arrived(rb2.at[j], (s, i, 3))
        top = both(j, chip, low) + rb1[j, 0, yy].astype(jnp.float32)
        top = top + rb2[j, 0].astype(jnp.float32)
        end = both(j, chip, high) + rb1[j, 1, xx].astype(jnp.float32)
        end = end + rb2[j, 1].astype(jnp.float32)
        if d:
            sb3[s, d - 1, low, :] = top.astype(jnp.bfloat16)
            sb3[s, d - 1, high, :] = end.astype(jnp.bfloat16)
            where = {"dp": partner(my_dp, d)}
            remote(sb3.at[s, d - 1], rb3.at[s, d - 1], where, thirds, (s, "over"))
        else:
            arrived(rb3.at[s], (s, "over"))
            for other in range(1, n_dp):
                top = top + rb3[s, other - 1, low, :].astype(jnp.float32)
                end = end + rb3[s, other - 1, high, :].astype(jnp.float32)
            mixed_ref[s * rows : s * rows + half, :] = top.astype(jnp.bfloat16)
            mixed_ref[s * rows + half : (s + 1) * rows, :] = end.astype(jnp.bfloat16)

    def gram():
        loaded(hx.at[0], hist_sem)
        loaded(hh.at[0], head_sem)
        arrived(hx.at[1:n_dp], "hist")
        arrived(hh.at[1:n_dp], "head")
        scale = 2.0 / (n_dp * hx.shape[1])

        @pl.loop(0, cols // tile)
        def _(n):
            at = pl.multiple_of(n * tile, tile)
            left = hx[:, :, pl.ds(at, tile)].reshape(n_dp * hx.shape[1], tile)
            right = hh[...].reshape(n_dp * hx.shape[1], HESS_COLS)
            product = lax.dot_general(
                left, right, (((0,), (0,)), ((), ())), preferred_element_type=jnp.float32
            )
            hess_ref[pl.ds(at, tile), :] = product * scale

    own(0, 0)
    own(0, 1)
    send_shares()
    history(2)
    own(0, 2)
    relay(0, 0)
    own(0, 3)
    own(1, 0)
    relay(0, 1)
    own(1, 1)
    corner(0, 0)
    relay(0, 2)
    own(1, 2)
    own(1, 3)
    widen(0, 0)
    corner(0, 1)
    widen(0, 1)
    relay(1, 0)
    corner(0, 2)
    arrive(0)
    widen(0, 2)
    relay(1, 1)
    widen(0, 3)
    activate(0)
    down(0, 0)
    corner(1, 0)
    history(1)
    history(3)
    relay(1, 2)
    down(0, 1)
    first(0, 0)
    corner(1, 1)
    down(0, 2)
    first(0, 1)
    corner(1, 2)
    widen(1, 0)
    first(0, 2)
    widen(1, 1)
    second(0, 0)
    widen(1, 2)
    arrive(1)
    second(0, 1)
    widen(1, 3)
    activate(1)
    down(1, 0)
    down(1, 1)
    first(1, 0)
    second(0, 2)
    third(0, 0)
    down(1, 2)
    first(1, 1)
    third(0, 1)
    down(0, 3)
    third(0, 2)
    down(1, 3)
    second(1, 0)
    first(1, 2)
    second(1, 1)
    first(0, 3)
    gram()
    third(1, 0)
    second(1, 2)
    first(1, 3)
    third(1, 1)
    second(0, 3)
    third(1, 2)
    second(1, 3)
    third(0, 3)
    third(1, 3)
    departed(mine.at[0 : mine.shape[0] - 1], gathers)
    departed(sb0, peers)
    departed(sb1, firsts)
    departed(sb2, seconds)
    departed(sb3, thirds)
    departed(hx.at[1:n_dp], hists)
    departed(hh.at[1:n_dp], heads)
    departed(share_all.at[1:n_expert], parts)


def store_kernel(mixed, hess, mixed_out, hess_out, sem):
    copies = [
        pltpu.make_async_copy(hess, hess_out, sem.at[0]),
        pltpu.make_async_copy(mixed, mixed_out, sem.at[1]),
    ]
    for copy in copies:
        copy.start()
    for copy in copies:
        copy.wait()


def everyone(tokens, routes, route_weight, w_gate, w_up, w_down, prev_inputs):
    total_rows, width = tokens.shape
    n_expert = lax.axis_size("expert")
    n_dp = lax.axis_size("dp")
    hidden_w = w_gate.shape[2]
    prev = prev_inputs.reshape(prev_inputs.shape[2], width)
    cols = width // n_dp
    chunks = 4
    depth = width // chunks
    chips = n_expert // 2
    rows = total_rows // SUBS
    half = rows // 2
    steps = SUBS * n_dp
    bf16, f32 = jnp.bfloat16, jnp.float32
    arrivals = SUBS * (4 * chunks - 2) + SUBS * (4 * n_dp + 1) + 3
    vmem = pl.BlockSpec(memory_space=pltpu.VMEM)
    hbm = pl.BlockSpec(memory_space=pl.ANY)
    mixed, hess = pl.pallas_call(
        functools.partial(dense_kernel, n_dp, n_expert),
        out_shape=(
            pltpu.VMEM((total_rows, cols), bf16),
            pltpu.VMEM((cols, HESS_COLS), f32),
        ),
        in_specs=[hbm] * 7,
        out_specs=(vmem, vmem),
        scratch_shapes=[
            pltpu.VMEM((SUBS, chunks, 2, chips, rows, depth), bf16),
            pltpu.VMEM((n_expert, n_expert, LANES), f32),
            pltpu.VMEM((chunks, depth, hidden_w), bf16),
            pltpu.VMEM((chunks, depth, hidden_w), bf16),
            pltpu.VMEM((n_dp, hidden_w, cols), bf16),
            pltpu.VMEM((n_expert * rows, hidden_w), f32),
            pltpu.VMEM((n_expert * rows, hidden_w), f32),
            pltpu.VMEM((SUBS, 2, chips * rows, hidden_w), bf16),
            pltpu.VMEM((steps, chips, rows, cols), f32),
            pltpu.VMEM((steps, chips, rows, cols), bf16),
            pltpu.VMEM((steps, chips, rows, cols), bf16),
            pltpu.VMEM((steps, 2, 2, half, cols), bf16),
            pltpu.VMEM((steps, 2, 2, half, cols), bf16),
            pltpu.VMEM((steps, 2, half, cols), bf16),
            pltpu.VMEM((steps, 2, half, cols), bf16),
            pltpu.VMEM((SUBS, n_dp - 1, rows, cols), bf16),
            pltpu.VMEM((SUBS, n_dp - 1, rows, cols), bf16),
            pltpu.VMEM((n_dp, prev.shape[0], cols), bf16),
            pltpu.VMEM((n_dp, prev.shape[0], HESS_COLS), bf16),
            pltpu.VMEM((routes.shape[1], total_rows), jnp.int32),
            pltpu.VMEM((routes.shape[1], total_rows), jnp.int32),
            pltpu.SemaphoreType.DMA((8,)),
            pltpu.SemaphoreType.DMA((8,)),
            pltpu.SemaphoreType.DMA((arrivals,)),
        ],
        compiler_params=pltpu.CompilerParams(
            collective_id=0, has_side_effects=True, vmem_limit_bytes=58000000
        ),
        name="dense_layer",
    )(tokens, routes.T, route_weight.T, w_gate[0], w_up[0], w_down[0], prev)
    mixed, hess = pl.pallas_call(
        store_kernel,
        out_shape=(
            jax.ShapeDtypeStruct(mixed.shape, bf16),
            jax.ShapeDtypeStruct(hess.shape, f32),
        ),
        in_specs=[vmem] * 2,
        out_specs=(hbm, hbm),
        scratch_shapes=[pltpu.SemaphoreType.DMA((2,))],
        compiler_params=pltpu.CompilerParams(vmem_limit_bytes=4194304),
        name="store_outputs",
    )(mixed, hess)
    return mixed, hess.reshape(cols, 1, HESS_COLS)


def shards(tokens, routes, route_weight, w_gate, w_up, w_down, prev_inputs):
    n_expert = lax.axis_size("expert")
    n_dp = lax.axis_size("dp")
    if w_gate.shape[0] == 1 and routes.shape[1] == n_expert == 2 * 2 * 2 and n_dp == 2 * 2:
        return everyone(tokens, routes, route_weight, w_gate, w_up, w_down, prev_inputs)
    hessian = gram_window(prev_inputs, n_dp, tokens.shape[1])
    return slotted(tokens, routes, route_weight, w_gate, w_up, w_down), hessian


def solution(mesh):
    placed = (
        P("expert", None),
        P("expert", None),
        P("expert", None),
        P("expert", None, "dp"),
        P("expert", None, "dp"),
        P("expert", "dp", None),
        P("dp", "expert", None, None),
    )
    return jax.shard_map(
        shards,
        mesh=mesh,
        in_specs=placed,
        out_specs=(P("expert", "dp"), P("dp", "expert", None)),
        check_vma=False,
    )
```

time: 96.8 us -> 67.5 us (0.70)
  Pallas kernels: 89 us -> 66.7 us
  local copies, waits for them, and re-layouts: 4.47 us -> 0 us
  other arithmetic: 2.22 us -> 0 us
    pallas_call x1, Pallas kernels: 89 us -> 65.7 us  [everyone(): pl.pallas_call(functools.partial(dense_kernel, n_dp, n_expert), out_shape...]
    unnamed x3 -> x0, local copies, waits for them, and re-layouts: 4.38 us -> none
    reduce_sum x2 -> x0, other arithmetic: 1.53 us -> none  [the longest x1 0.82 us: everyone(): by_expert = jnp.sum(jnp.where(named, shares[:, :, None], 0.0), axis=1)]
    pallas_call x0 -> x1, Pallas kernels: none -> 1.01 us  [everyone(): pl.pallas_call(store_kernel, out_shape=(jax.ShapeDtypeStruct(mixed.shape,...]
where the time goes in v1:
time: 67.5 us; the launch traced here: 67.3 us
  Pallas kernels  66.7 us (99%)
    pallas_call x1, Pallas kernels, everyone(): pl.pallas_call(functools.partial(dense_kernel, n_dp, n_expert), out_shape...  65.7 us

profile of v1, /device:TPU:0, one launch (start us, length us, event | category | flops | bytes accessed | tf_op | source)
XLA Modules:
  0.0 67.3 jit_solution(13211224808091768497)
XLA Ops:
  0.6 65.7 %dense_layer.1 = (bf16[64,1792]{1,0:T(8,128)(2,1)S(1)}, f32[1792,128]{1,0:T(8,128)S(1)}) custom-call(bf16[64,7168]{1,0:T(8,128)(2,1)} %tokens.1, s32[8,64]{1,0:T(8,128)} %bitcast.13, s32[8,64]{1,0:T(8,128)} %bitcast.14, bf16[7168,512]{1,0:T(8,128)(2,1)} %bitcast.9, bf16[7168,512]{1,0:T(8,128)(2,1)} %bitcast.10, bf16[512,7168]{1,0:T(8,128)(2,1)} %bitcast.11, ...), custom_call_target="tpu_custom_call" | custom-call | tf_op jit(solution)/shard_map/dense_layer/pallas_call | solution.py:498
  66.3 1.0 %store_outputs.1 = (bf16[64,1792]{1,0:T(8,128)(2,1)}, f32[1792,128]{1,0:T(8,128)}) custom-call(bf16[64,1792]{1,0:T(8,128)(2,1)S(1)} %get-tuple-element.6.mixed, f32[1792,128]{1,0:T(8,128)S(1)} %get-tuple-element.7.hess), custom_call_target="tpu_custom_call" | custom-call | tf_op jit(solution)/shard_map/store_outputs/pallas_call | solution.py:537

commit v2 on v1

--- a/solution.py
+++ b/solution.py
@@ -133,6 +133,7 @@
     lsem,
     send_sem,
     recv_sem,
+    round_sem,
 ):
     me = lax.axis_index("expert")
     my_dp = lax.axis_index("dp")
@@ -192,26 +193,45 @@
     for c in range(chunks):
         local(w_gate.at[piece(c), :], wg.at[c], gate_sem)
         local(w_up.at[piece(c), :], wu.at[c], up_sem)
-    turns = list(range(n_dp - 1, -1, -1))
-    for i, d in enumerate(turns):
-        start = pl.multiple_of(partner(my_dp, d) * cols, LANES)
+    pair = my_dp // 2
+    inner = (my_dp + pair) % 2
+    turns = [
+        ((n_dp - 1) * (1 - pair), 3 - inner),
+        (n_dp // 2 - pair, 2 + inner),
+        (flip(my_dp, 1), 1),
+        (my_dp, 0),
+    ]
+    for i, (owner, _) in enumerate(turns):
+        start = pl.multiple_of(owner * cols, LANES)
         local(w_down.at[:, pl.ds(start, cols)], wd.at[i], down_sem)
     local(prev.at[:, pl.ds(pl.multiple_of(my_dp * cols, LANES), cols)], hx.at[0], hist_sem)
     local(prev.at[:, 0:HESS_COLS], hh.at[0], head_sem)
 
+    to_peer, to_x, to_y = {"expert": peer}, {"expert": ex}, {"expert": ey}
+    has_lower = (my_dp + n_dp - 1) // n_dp
+    has_upper = (n_dp - 1 - my_dp + n_dp - 1) // n_dp
+
+    def greet(sem):
+        for where in (to_peer, to_x, to_y):
+            pl.semaphore_signal(sem, inc=1, device_id=where, device_id_type=MESH)
+        for exists, where in ((has_lower, my_dp - 1), (has_upper, my_dp + 1)):
+
+            @pl.when(exists == 1)
+            def _():
+                pl.semaphore_signal(sem, inc=1, device_id={"dp": where}, device_id_type=MESH)
+
+    def met(sem):
+        pl.semaphore_wait(sem, 3 + has_lower + has_upper)
+
+    def rounds(n):
+        greet(round_sem.at[n])
+        met(round_sem.at[n])
+
     barrier = pltpu.get_barrier_semaphore()
-    for d in range(1, n_expert):
-        pl.semaphore_signal(
-            barrier, inc=1, device_id={"expert": (me + d) % n_expert}, device_id_type=MESH
-        )
-    for d in range(1, n_dp):
-        pl.semaphore_signal(
-            barrier, inc=1, device_id={"dp": partner(my_dp, d)}, device_id_type=MESH
-        )
-    pl.semaphore_wait(barrier, n_expert + n_dp - 2)
+    greet(barrier)
+    met(barrier)
 
     to_z = {"dp": flip(my_dp, 1)}
-    to_peer, to_x, to_y = {"expert": peer}, {"expert": ex}, {"expert": ey}
 
     def block(s, c, who):
         return xall.at[s, c, who % 2, who // 2]
@@ -288,11 +308,13 @@
         for d in range(1, n_expert):
             remote(here, here, {"expert": (me + d) % n_expert}, parts, "shares")
 
-    def history(d):
+    def history(d, first_half=True, second_half=True):
+        count = hx.shape[1]
+        take = slice(0 if first_half else count // 2, count if second_half else count // 2)
         start = pl.multiple_of(partner(my_dp, d) * cols, LANES)
         where = {"dp": partner(my_dp, d)}
-        remote(prev.at[:, pl.ds(start, cols)], hx.at[d], where, hists, "hist")
-        remote(prev.at[:, 0:HESS_COLS], hh.at[d], where, heads, "head")
+        remote(prev.at[take, pl.ds(start, cols)], hx.at[d, take], where, hists, "hist")
+        remote(prev.at[take, 0:HESS_COLS], hh.at[d, take], where, heads, "head")
 
     def activate(s):
         if s == 0:
@@ -351,18 +373,17 @@
 
     def third(s, i):
         j = s * n_dp + i
-        d = turns[i]
+        owner, mask = turns[i]
         chip = me // 2
         arrived(rb2.at[j], (s, i, 3))
         top = both(j, chip, low) + rb1[j, 0, yy].astype(jnp.float32)
         top = top + rb2[j, 0].astype(jnp.float32)
         end = both(j, chip, high) + rb1[j, 1, xx].astype(jnp.float32)
         end = end + rb2[j, 1].astype(jnp.float32)
-        if d:
-            sb3[s, d - 1, low, :] = top.astype(jnp.bfloat16)
-            sb3[s, d - 1, high, :] = end.astype(jnp.bfloat16)
-            where = {"dp": partner(my_dp, d)}
-            remote(sb3.at[s, d - 1], rb3.at[s, d - 1], where, thirds, (s, "over"))
+        if i < n_dp - 1:
+            sb3[s, i, low, :] = top.astype(jnp.bfloat16)
+            sb3[s, i, high, :] = end.astype(jnp.bfloat16)
+            remote(sb3.at[s, i], rb3.at[s, mask - 1], {"dp": owner}, thirds, (s, "over"))
         else:
             arrived(rb3.at[s], (s, "over"))
             for other in range(1, n_dp):
@@ -390,68 +411,70 @@
 
     own(0, 0)
     own(0, 1)
+    own(0, 2)
+    rounds(0)
+    history(2)
+    rounds(1)
     send_shares()
-    history(2)
-    own(0, 2)
     relay(0, 0)
     own(0, 3)
+    relay(0, 1)
     own(1, 0)
-    relay(0, 1)
+    relay(0, 2)
     own(1, 1)
     corner(0, 0)
-    relay(0, 2)
+    corner(0, 1)
+    widen(0, 0)
+    widen(0, 1)
+    relay(1, 0)
     own(1, 2)
     own(1, 3)
-    widen(0, 0)
-    corner(0, 1)
-    widen(0, 1)
-    relay(1, 0)
     corner(0, 2)
     arrive(0)
     widen(0, 2)
     relay(1, 1)
     widen(0, 3)
+    corner(1, 0)
     activate(0)
     down(0, 0)
-    corner(1, 0)
+    down(0, 1)
+    relay(1, 2)
+    first(0, 0)
+    history(3)
     history(1)
-    history(3)
-    relay(1, 2)
-    down(0, 1)
-    first(0, 0)
-    corner(1, 1)
     down(0, 2)
     first(0, 1)
-    corner(1, 2)
+    corner(1, 1)
     widen(1, 0)
     first(0, 2)
     widen(1, 1)
+    corner(1, 2)
+    arrive(1)
+    widen(1, 2)
+    widen(1, 3)
     second(0, 0)
-    widen(1, 2)
-    arrive(1)
-    second(0, 1)
-    widen(1, 3)
     activate(1)
     down(1, 0)
     down(1, 1)
+    second(0, 1)
     first(1, 0)
+    down(1, 2)
     second(0, 2)
+    first(1, 1)
     third(0, 0)
-    down(1, 2)
-    first(1, 1)
+    down(1, 3)
     third(0, 1)
     down(0, 3)
-    third(0, 2)
-    down(1, 3)
     second(1, 0)
     first(1, 2)
+    third(0, 2)
     second(1, 1)
+    third(1, 0)
     first(0, 3)
     gram()
-    third(1, 0)
     second(1, 2)
+    third(1, 1)
     first(1, 3)
-    third(1, 1)
     second(0, 3)
     third(1, 2)
     second(1, 3)
@@ -528,6 +551,7 @@
             pltpu.SemaphoreType.DMA((8,)),
             pltpu.SemaphoreType.DMA((8,)),
             pltpu.SemaphoreType.DMA((arrivals,)),
+            pltpu.SemaphoreType.REGULAR((2,)),
         ],
         compiler_params=pltpu.CompilerParams(
             collective_id=0, has_side_effects=True, vmem_limit_bytes=58000000

time: 67.5 us -> 62.6 us (0.927)
  Pallas kernels: 66.7 us -> 61.7 us
    pallas_call x1, Pallas kernels: 65.7 us -> 60.7 us  [everyone(): pl.pallas_call(functools.partial(dense_kernel, n_dp, n_expert), out_shape...]
where the time goes in v2:
time: 62.6 us; the launch traced here: 62.3 us
  Pallas kernels  61.7 us (99%)
  between operations  0.64 us (1%)
    pallas_call x1, Pallas kernels, everyone(): pl.pallas_call(functools.partial(dense_kernel, n_dp, n_expert), out_shape...  60.7 us

profile of v2, /device:TPU:0, one launch (start us, length us, event | category | flops | bytes accessed | tf_op | source)
XLA Modules:
  0.0 62.3 jit_solution(2953614339920785571)
XLA Ops:
  0.6 60.7 %dense_layer.1 = (bf16[64,1792]{1,0:T(8,128)(2,1)S(1)}, f32[1792,128]{1,0:T(8,128)S(1)}) custom-call(bf16[64,7168]{1,0:T(8,128)(2,1)} %tokens.1, s32[8,64]{1,0:T(8,128)} %bitcast.13, s32[8,64]{1,0:T(8,128)} %bitcast.14, bf16[7168,512]{1,0:T(8,128)(2,1)} %bitcast.9, bf16[7168,512]{1,0:T(8,128)(2,1)} %bitcast.10, bf16[512,7168]{1,0:T(8,128)(2,1)} %bitcast.11, ...), custom_call_target="tpu_custom_call" | custom-call | tf_op jit(solution)/shard_map/dense_layer/pallas_call | solution.py:521
  61.3 1.0 %store_outputs.1 = (bf16[64,1792]{1,0:T(8,128)(2,1)}, f32[1792,128]{1,0:T(8,128)}) custom-call(bf16[64,1792]{1,0:T(8,128)(2,1)S(1)} %get-tuple-element.6.mixed, f32[1792,128]{1,0:T(8,128)S(1)} %get-tuple-element.7.hess), custom_call_target="tpu_custom_call" | custom-call | tf_op jit(solution)/shard_map/store_outputs/pallas_call | solution.py:561

commit v3 on v2

--- a/solution.py
+++ b/solution.py
@@ -193,12 +193,12 @@
     for c in range(chunks):
         local(w_gate.at[piece(c), :], wg.at[c], gate_sem)
         local(w_up.at[piece(c), :], wu.at[c], up_sem)
-    pair = my_dp // 2
-    inner = (my_dp + pair) % 2
+    odd = my_dp % 2
+    inner = (my_dp + my_dp // 2) % 2
     turns = [
-        ((n_dp - 1) * (1 - pair), 3 - inner),
-        (n_dp // 2 - pair, 2 + inner),
-        (flip(my_dp, 1), 1),
+        ((n_dp - 1) * (1 - odd), 3 - 2 * inner),
+        (flip(my_dp, 2), 2),
+        (1 + odd, 1 + 2 * inner),
         (my_dp, 0),
     ]
     for i, (owner, _) in enumerate(turns):
@@ -347,50 +347,61 @@
             mine[j, :, :, at] = out[1]
         remote(sb0.at[j], rb0.at[j], to_peer, peers, (s, i, 0))
 
-    def both(j, chip, part):
-        return mine[j, chip, part, :] + rb0[j, chip, part, :].astype(jnp.float32)
-
-    def first(s, i):
-        j = s * n_dp + i
-        arrived(rb0.at[j], (s, i, 0))
+    cuts = {(subs - 1, n_dp - 2): cols // tile // 2 * tile, (subs - 1, n_dp - 1): cols - 2 * tile}
+
+    def columns(s, i, part):
+        cut = cuts.get((s, i), cols)
+        return slice(cut, cols) if part else slice(0, cut)
+
+    def both(j, chip, part, at):
+        return mine[j, chip, part, at] + rb0[j, chip, part, at].astype(jnp.float32)
+
+    def first(s, i, part=0):
+        j, at = s * n_dp + i, columns(s, i, part)
+        if not part:
+            arrived(rb0.at[j], (s, i, 0))
         for k in range(2):
-            sb1[j, 0, k] = both(j, k * 2 + 1 - xx, low).astype(jnp.bfloat16)
-        remote(sb1.at[j, 0], rb1.at[j, 0], to_x, firsts, (s, i, 1))
+            sb1[j, 0, k, :, at] = both(j, k * 2 + 1 - xx, low, at).astype(jnp.bfloat16)
+        source, target = sb1.at[j, 0, :, :, at], rb1.at[j, 0, :, :, at]
+        remote(source, target, to_x, firsts, (s, i, 1, part))
         for k in range(2):
-            sb1[j, 1, k] = both(j, (1 - yy) * 2 + k, high).astype(jnp.bfloat16)
-        remote(sb1.at[j, 1], rb1.at[j, 1], to_y, firsts, (s, i, 2))
-
-    def second(s, i):
-        j = s * n_dp + i
-        arrived(rb1.at[j, 0], (s, i, 1))
-        out = both(j, (1 - yy) * 2 + xx, low) + rb1[j, 0, 1 - yy].astype(jnp.float32)
-        sb2[j, 0] = out.astype(jnp.bfloat16)
-        remote(sb2.at[j, 0], rb2.at[j, 0], to_y, seconds, (s, i, 3))
-        arrived(rb1.at[j, 1], (s, i, 2))
-        out = both(j, yy * 2 + 1 - xx, high) + rb1[j, 1, 1 - xx].astype(jnp.float32)
-        sb2[j, 1] = out.astype(jnp.bfloat16)
-        remote(sb2.at[j, 1], rb2.at[j, 1], to_x, seconds, (s, i, 3))
-
-    def third(s, i):
-        j = s * n_dp + i
+            sb1[j, 1, k, :, at] = both(j, (1 - yy) * 2 + k, high, at).astype(jnp.bfloat16)
+        source, target = sb1.at[j, 1, :, :, at], rb1.at[j, 1, :, :, at]
+        remote(source, target, to_y, firsts, (s, i, 2, part))
+
+    def second(s, i, part=0):
+        j, at = s * n_dp + i, columns(s, i, part)
+        arrived(rb1.at[j, 0, :, :, at], (s, i, 1, part))
+        out = both(j, (1 - yy) * 2 + xx, low, at) + rb1[j, 0, 1 - yy, :, at].astype(jnp.float32)
+        sb2[j, 0, :, at] = out.astype(jnp.bfloat16)
+        remote(sb2.at[j, 0, :, at], rb2.at[j, 0, :, at], to_y, seconds, (s, i, 3, part))
+        arrived(rb1.at[j, 1, :, :, at], (s, i, 2, part))
+        out = both(j, yy * 2 + 1 - xx, high, at) + rb1[j, 1, 1 - xx, :, at].astype(jnp.float32)
+        sb2[j, 1, :, at] = out.astype(jnp.bfloat16)
+        remote(sb2.at[j, 1, :, at], rb2.at[j, 1, :, at], to_x, seconds, (s, i, 3, part))
+
+    def third(s, i, part=0):
+        j, at = s * n_dp + i, columns(s, i, part)
         owner, mask = turns[i]
         chip = me // 2
-        arrived(rb2.at[j], (s, i, 3))
-        top = both(j, chip, low) + rb1[j, 0, yy].astype(jnp.float32)
-        top = top + rb2[j, 0].astype(jnp.float32)
-        end = both(j, chip, high) + rb1[j, 1, xx].astype(jnp.float32)
-        end = end + rb2[j, 1].astype(jnp.float32)
+        if i == n_dp - 1 and not part:
+            arrived(rb3.at[s], (s, "over"))
+        arrived(rb2.at[j, :, :, at], (s, i, 3, part))
+        top = both(j, chip, low, at) + rb1[j, 0, yy, :, at].astype(jnp.float32)
+        top = top + rb2[j, 0, :, at].astype(jnp.float32)
+        end = both(j, chip, high, at) + rb1[j, 1, xx, :, at].astype(jnp.float32)
+        end = end + rb2[j, 1, :, at].astype(jnp.float32)
         if i < n_dp - 1:
-            sb3[s, i, low, :] = top.astype(jnp.bfloat16)
-            sb3[s, i, high, :] = end.astype(jnp.bfloat16)
-            remote(sb3.at[s, i], rb3.at[s, mask - 1], {"dp": owner}, thirds, (s, "over"))
+            sb3[s, i, low, at] = top.astype(jnp.bfloat16)
+            sb3[s, i, high, at] = end.astype(jnp.bfloat16)
+            source, target = sb3.at[s, i, :, at], rb3.at[s, mask - 1, :, at]
+            remote(source, target, {"dp": owner}, thirds, (s, "over"))
         else:
-            arrived(rb3.at[s], (s, "over"))
             for other in range(1, n_dp):
-                top = top + rb3[s, other - 1, low, :].astype(jnp.float32)
-                end = end + rb3[s, other - 1, high, :].astype(jnp.float32)
-            mixed_ref[s * rows : s * rows + half, :] = top.astype(jnp.bfloat16)
-            mixed_ref[s * rows + half : (s + 1) * rows, :] = end.astype(jnp.bfloat16)
+                top = top + rb3[s, other - 1, low, at].astype(jnp.float32)
+                end = end + rb3[s, other - 1, high, at].astype(jnp.float32)
+            mixed_ref[s * rows : s * rows + half, at] = top.astype(jnp.bfloat16)
+            mixed_ref[s * rows + half : (s + 1) * rows, at] = end.astype(jnp.bfloat16)
 
     def gram():
         loaded(hx.at[0], hist_sem)
@@ -424,6 +435,10 @@
     own(1, 1)
     corner(0, 0)
     corner(0, 1)
+    @pl.when(inner == 1)
+    def _():
+        history(3)
+
     widen(0, 0)
     widen(0, 1)
     relay(1, 0)
@@ -440,7 +455,6 @@
     down(0, 1)
     relay(1, 2)
     first(0, 0)
-    history(3)
     history(1)
     down(0, 2)
     first(0, 1)
@@ -450,6 +464,10 @@
     widen(1, 1)
     corner(1, 2)
     arrive(1)
+    @pl.when(inner == 0)
+    def _():
+        history(3)
+
     widen(1, 2)
     widen(1, 3)
     second(0, 0)
@@ -466,20 +484,26 @@
     third(0, 1)
     down(0, 3)
     second(1, 0)
-    first(1, 2)
+    first(1, 2, 0)
+    first(1, 2, 1)
     third(0, 2)
     second(1, 1)
     third(1, 0)
     first(0, 3)
     gram()
-    second(1, 2)
+    second(1, 2, 0)
+    second(1, 2, 1)
     third(1, 1)
-    first(1, 3)
+    first(1, 3, 0)
+    first(1, 3, 1)
     second(0, 3)
-    third(1, 2)
-    second(1, 3)
+    third(1, 2, 0)
+    third(1, 2, 1)
+    second(1, 3, 0)
+    second(1, 3, 1)
     third(0, 3)
-    third(1, 3)
+    third(1, 3, 0)
+    third(1, 3, 1)
     departed(mine.at[0 : mine.shape[0] - 1], gathers)
     departed(sb0, peers)
     departed(sb1, firsts)
@@ -515,7 +539,7 @@
     half = rows // 2
     steps = SUBS * n_dp
     bf16, f32 = jnp.bfloat16, jnp.float32
-    arrivals = SUBS * (4 * chunks - 2) + SUBS * (4 * n_dp + 1) + 3
+    arrivals = SUBS * (4 * chunks - 2) + SUBS * (4 * n_dp + 1) + 3 + 2 * 3
     vmem = pl.BlockSpec(memory_space=pltpu.VMEM)
     hbm = pl.BlockSpec(memory_space=pl.ANY)
     mixed, hess = pl.pallas_call(

time: 62.6 us -> 61.7 us (0.986)
  Pallas kernels: 61.7 us -> 60.9 us
    pallas_call x1, Pallas kernels: 60.7 us -> 59.9 us  [everyone(): pl.pallas_call(functools.partial(dense_kernel, n_dp, n_expert), out_shape...]
where the time goes in v3:
time: 61.7 us; the launch traced here: 61.5 us
  Pallas kernels  60.9 us (99%)
  between operations  0.64 us (1%)
    pallas_call x1, Pallas kernels, everyone(): pl.pallas_call(functools.partial(dense_kernel, n_dp, n_expert), out_shape...  59.9 us

profile of v3, /device:TPU:0, one launch (start us, length us, event | category | flops | bytes accessed | tf_op | source)
XLA Modules:
  0.0 61.5 jit_solution(6128918703925708112)
XLA Ops:
  0.6 59.9 %dense_layer.1 = (bf16[64,1792]{1,0:T(8,128)(2,1)S(1)}, f32[1792,128]{1,0:T(8,128)S(1)}) custom-call(bf16[64,7168]{1,0:T(8,128)(2,1)} %tokens.1, s32[8,64]{1,0:T(8,128)} %bitcast.13, s32[8,64]{1,0:T(8,128)} %bitcast.14, bf16[7168,512]{1,0:T(8,128)(2,1)} %bitcast.9, bf16[7168,512]{1,0:T(8,128)(2,1)} %bitcast.10, bf16[512,7168]{1,0:T(8,128)(2,1)} %bitcast.11, ...), custom_call_target="tpu_custom_call" | custom-call | tf_op jit(solution)/shard_map/dense_layer/pallas_call | solution.py:545
  60.5 1.0 %store_outputs.1 = (bf16[64,1792]{1,0:T(8,128)(2,1)}, f32[1792,128]{1,0:T(8,128)}) custom-call(bf16[64,1792]{1,0:T(8,128)(2,1)S(1)} %get-tuple-element.6.mixed, f32[1792,128]{1,0:T(8,128)S(1)} %get-tuple-element.7.hess), custom_call_target="tpu_custom_call" | custom-call | tf_op jit(solution)/shard_map/store_outputs/pallas_call | solution.py:585

commit v4 on v3

--- a/solution.py
+++ b/solution.py
@@ -146,8 +146,31 @@
     chips = n_expert // 2
     cols = rb3.shape[-1]
     hidden_w = wg.shape[-1]
+    to_peer, to_x, to_y = {"expert": peer}, {"expert": ex}, {"expert": ey}
+    has_lower = (my_dp + n_dp - 1) // n_dp
+    has_upper = (n_dp - 1 - my_dp + n_dp - 1) // n_dp
+
+    def greet(sem):
+        for where in (to_peer, to_x, to_y):
+            pl.semaphore_signal(sem, inc=1, device_id=where, device_id_type=MESH)
+        for exists, where in ((has_lower, my_dp - 1), (has_upper, my_dp + 1)):
+
+            @pl.when(exists == 1)
+            def _():
+                pl.semaphore_signal(sem, inc=1, device_id={"dp": where}, device_id_type=MESH)
+
+    def met(sem):
+        pl.semaphore_wait(sem, 3 + has_lower + has_upper)
+
+    def rounds(n):
+        greet(round_sem.at[n])
+        met(round_sem.at[n])
+
+    barrier = pltpu.get_barrier_semaphore()
+    greet(barrier)
+
     tokens_sem, gate_sem, up_sem, down_sem, hist_sem, head_sem, ids_sem, counts_sem = range(8)
-    gathers, peers, firsts, seconds, thirds, hists, heads, parts = range(8)
+    gathers, sums, thirds, hists, heads, parts = range(6)
     lanes = {}
 
     def local(src, dst, sem):
@@ -196,8 +219,8 @@
     odd = my_dp % 2
     inner = (my_dp + my_dp // 2) % 2
     turns = [
-        ((n_dp - 1) * (1 - odd), 3 - 2 * inner),
-        (flip(my_dp, 2), 2),
+        ((n_dp - 1) * (1 - my_dp // 2), 3 - inner),
+        (flip(my_dp, 2) * (1 - inner) + flip(my_dp, 1) * inner, 2 - inner),
         (1 + odd, 1 + 2 * inner),
         (my_dp, 0),
     ]
@@ -207,28 +230,6 @@
     local(prev.at[:, pl.ds(pl.multiple_of(my_dp * cols, LANES), cols)], hx.at[0], hist_sem)
     local(prev.at[:, 0:HESS_COLS], hh.at[0], head_sem)
 
-    to_peer, to_x, to_y = {"expert": peer}, {"expert": ex}, {"expert": ey}
-    has_lower = (my_dp + n_dp - 1) // n_dp
-    has_upper = (n_dp - 1 - my_dp + n_dp - 1) // n_dp
-
-    def greet(sem):
-        for where in (to_peer, to_x, to_y):
-            pl.semaphore_signal(sem, inc=1, device_id=where, device_id_type=MESH)
-        for exists, where in ((has_lower, my_dp - 1), (has_upper, my_dp + 1)):
-
-            @pl.when(exists == 1)
-            def _():
-                pl.semaphore_signal(sem, inc=1, device_id={"dp": where}, device_id_type=MESH)
-
-    def met(sem):
-        pl.semaphore_wait(sem, 3 + has_lower + has_upper)
-
-    def rounds(n):
-        greet(round_sem.at[n])
-        met(round_sem.at[n])
-
-    barrier = pltpu.get_barrier_semaphore()
-    greet(barrier)
     met(barrier)
 
     to_z = {"dp": flip(my_dp, 1)}
@@ -345,9 +346,11 @@
             out = out.reshape(2, chips, rows, tile)
             sb0[j, :, :, at] = out[0].astype(jnp.bfloat16)
             mine[j, :, :, at] = out[1]
-        remote(sb0.at[j], rb0.at[j], to_peer, peers, (s, i, 0))
-
-    cuts = {(subs - 1, n_dp - 2): cols // tile // 2 * tile, (subs - 1, n_dp - 1): cols - 2 * tile}
+        remote(sb0.at[j], rb0.at[j], to_peer, sums, (s, i, 0))
+
+    middle = cols // tile // 2 * tile
+    cuts = {(s, n_dp - 2): middle for s in range(subs)}
+    cuts[subs - 1, n_dp - 1] = cols - 2 * tile
 
     def columns(s, i, part):
         cut = cuts.get((s, i), cols)
@@ -363,22 +366,22 @@
         for k in range(2):
             sb1[j, 0, k, :, at] = both(j, k * 2 + 1 - xx, low, at).astype(jnp.bfloat16)
         source, target = sb1.at[j, 0, :, :, at], rb1.at[j, 0, :, :, at]
-        remote(source, target, to_x, firsts, (s, i, 1, part))
+        remote(source, target, to_x, sums, (s, i, 1, part))
         for k in range(2):
             sb1[j, 1, k, :, at] = both(j, (1 - yy) * 2 + k, high, at).astype(jnp.bfloat16)
         source, target = sb1.at[j, 1, :, :, at], rb1.at[j, 1, :, :, at]
-        remote(source, target, to_y, firsts, (s, i, 2, part))
+        remote(source, target, to_y, sums, (s, i, 2, part))
 
     def second(s, i, part=0):
         j, at = s * n_dp + i, columns(s, i, part)
         arrived(rb1.at[j, 0, :, :, at], (s, i, 1, part))
         out = both(j, (1 - yy) * 2 + xx, low, at) + rb1[j, 0, 1 - yy, :, at].astype(jnp.float32)
         sb2[j, 0, :, at] = out.astype(jnp.bfloat16)
-        remote(sb2.at[j, 0, :, at], rb2.at[j, 0, :, at], to_y, seconds, (s, i, 3, part))
+        remote(sb2.at[j, 0, :, at], rb2.at[j, 0, :, at], to_y, sums, (s, i, 3, part))
         arrived(rb1.at[j, 1, :, :, at], (s, i, 2, part))
         out = both(j, yy * 2 + 1 - xx, high, at) + rb1[j, 1, 1 - xx, :, at].astype(jnp.float32)
         sb2[j, 1, :, at] = out.astype(jnp.bfloat16)
-        remote(sb2.at[j, 1, :, at], rb2.at[j, 1, :, at], to_x, seconds, (s, i, 3, part))
+        remote(sb2.at[j, 1, :, at], rb2.at[j, 1, :, at], to_x, sums, (s, i, 3, part))
 
     def third(s, i, part=0):
         j, at = s * n_dp + i, columns(s, i, part)
@@ -460,7 +463,7 @@
     first(0, 1)
     corner(1, 1)
     widen(1, 0)
-    first(0, 2)
+    first(0, 2, 0)
     widen(1, 1)
     corner(1, 2)
     arrive(1)
@@ -469,24 +472,27 @@
         history(3)
 
     widen(1, 2)
+    second(0, 0)
+    first(0, 2, 1)
     widen(1, 3)
-    second(0, 0)
     activate(1)
     down(1, 0)
     down(1, 1)
     second(0, 1)
     first(1, 0)
+    third(0, 0)
     down(1, 2)
-    second(0, 2)
+    second(0, 2, 0)
+    second(0, 2, 1)
     first(1, 1)
-    third(0, 0)
+    third(0, 1)
     down(1, 3)
-    third(0, 1)
     down(0, 3)
     second(1, 0)
     first(1, 2, 0)
     first(1, 2, 1)
-    third(0, 2)
+    third(0, 2, 0)
+    third(0, 2, 1)
     second(1, 1)
     third(1, 0)
     first(0, 3)
@@ -505,9 +511,7 @@
     third(1, 3, 0)
     third(1, 3, 1)
     departed(mine.at[0 : mine.shape[0] - 1], gathers)
-    departed(sb0, peers)
-    departed(sb1, firsts)
-    departed(sb2, seconds)
+    departed(mine.at[0 : mine.shape[0] - 1], sums)
     departed(sb3, thirds)
     departed(hx.at[1:n_dp], hists)
     departed(hh.at[1:n_dp], heads)
@@ -539,7 +543,7 @@
     half = rows // 2
     steps = SUBS * n_dp
     bf16, f32 = jnp.bfloat16, jnp.float32
-    arrivals = SUBS * (4 * chunks - 2) + SUBS * (4 * n_dp + 1) + 3 + 2 * 3
+    arrivals = SUBS * (4 * chunks - 2) + SUBS * (4 * n_dp + 1) + 3 + 3 * 3
     vmem = pl.BlockSpec(memory_space=pltpu.VMEM)
     hbm = pl.BlockSpec(memory_space=pl.ANY)
     mixed, hess = pl.pallas_call(
@@ -573,7 +577,7 @@
             pltpu.VMEM((routes.shape[1], total_rows), jnp.int32),
             pltpu.VMEM((routes.shape[1], total_rows), jnp.int32),
             pltpu.SemaphoreType.DMA((8,)),
-            pltpu.SemaphoreType.DMA((8,)),
+            pltpu.SemaphoreType.DMA((6,)),
             pltpu.SemaphoreType.DMA((arrivals,)),
             pltpu.SemaphoreType.REGULAR((2,)),
         ],

time: 61.7 us -> 61.7 us (level)
  no operation moved by 1% of the time
where the time goes in v4:
time: 61.7 us; the launch traced here: 61.5 us
  Pallas kernels  60.9 us (99%)
  between operations  0.64 us (1%)
    pallas_call x1, Pallas kernels, everyone(): pl.pallas_call(functools.partial(dense_kernel, n_dp, n_expert), out_shape...  59.9 us

profile of v4, /device:TPU:0, one launch (start us, length us, event | category | flops | bytes accessed | tf_op | source)
XLA Modules:
  0.0 61.5 jit_solution(13800970057143553963)
XLA Ops:
  0.6 59.9 %dense_layer.1 = (bf16[64,1792]{1,0:T(8,128)(2,1)S(1)}, f32[1792,128]{1,0:T(8,128)S(1)}) custom-call(bf16[64,7168]{1,0:T(8,128)(2,1)} %tokens.1, s32[8,64]{1,0:T(8,128)} %bitcast.13, s32[8,64]{1,0:T(8,128)} %bitcast.14, bf16[7168,512]{1,0:T(8,128)(2,1)} %bitcast.9, bf16[7168,512]{1,0:T(8,128)(2,1)} %bitcast.10, bf16[512,7168]{1,0:T(8,128)(2,1)} %bitcast.11, ...), custom_call_target="tpu_custom_call" | custom-call | tf_op jit(solution)/shard_map/dense_layer/pallas_call | solution.py:549
  60.5 1.0 %store_outputs.1 = (bf16[64,1792]{1,0:T(8,128)(2,1)}, f32[1792,128]{1,0:T(8,128)}) custom-call(bf16[64,1792]{1,0:T(8,128)(2,1)S(1)} %get-tuple-element.6.mixed, f32[1792,128]{1,0:T(8,128)S(1)} %get-tuple-element.7.hess), custom_call_target="tpu_custom_call" | custom-call | tf_op jit(solution)/shard_map/store_outputs/pallas_call | solution.py:589
